TPU v7x, 512 devices: a whole 4x8x8 slice. The times are simulated.
512 devices in a mesh: col: 64 (over y_hi, x, z), tok: 8 (over y_lo, core).
Axes of the slice: x: 4, y: 8 (y_hi: 2, y_lo: 4; y = y_hi * 4 + y_lo), z: 8, core: 2. Of those that a mesh axis runs over, the one named last changes fastest.
Arguments:
- acts: bfloat16 [2048, 8192], P('tok', 'col'), may hold values from -6 to 6
- grad_out: bfloat16 [2048, 8192], P('tok', 'col'), may hold values from -0.19921875 to 0.19921875
- left_factor: float32 [8, 8192, 1024], P('tok', 'col'), may hold values from -6 to 6
- right_factor: float32 [8, 8192, 1024], P('tok', 'col'), may hold values from -6 to 6
- left_basis: bfloat16 [8, 8192, 1024], P('tok', 'col'), may hold values from -0.1875 to 0.1875
- right_basis: bfloat16 [8, 8192, 1024], P('tok', 'col'), may hold values from -0.1875 to 0.1875
- moment: float32 [8192, 8192], P('tok', 'col'), may hold values from -2 to 2
- second: float32 [8192, 8192], P('tok', 'col'), may hold values from 0.05 to 2
Outputs:
- left_out: float32 [8, 8192, 1024], P('tok', 'col')
- right_out: float32 [8, 8192, 1024], P('tok', 'col')
- moment_out: float32 [8192, 8192], P('tok', 'col')
- second_out: float32 [8192, 8192], P('tok', 'col')
- update: bfloat16 [8192, 8192], P('tok', 'col')
All inputs are finite; a program needn't handle non-finite values.
Results may differ from a plain program's by a relative error of at most 0.0075.
Values may be sent and summed in bfloat16 or wider, within the bound.
A program may use at most 64 MiB of HBM per device.

v0:
```python
import jax
import jax.numpy as jnp
from jax import lax
from jax.sharding import PartitionSpec as P

B = 1024
shampoo_beta = 0.95
first_beta = 0.9
second_beta = 0.95
first_corr = 1.0 - 0.9**4
second_corr = 1.0 - 0.95**4
epsilon = 1e-08


def swapped(array, axis, distance):
    return lax.ppermute(array, axis, [(i, i ^ 1 << distance) for i in range(lax.axis_size(axis))])


def join_pair(current, incoming, axis, lower):
    width = current.shape[axis]
    shape = list(current.shape)
    shape[axis] = 2 * width
    joined = jnp.zeros(shape, current.dtype)
    mine_at = jnp.where(lower, 0, width)
    theirs_at = width - mine_at
    joined = lax.dynamic_update_slice_in_dim(joined, current, mine_at, axis)
    return lax.dynamic_update_slice_in_dim(joined, incoming, theirs_at, axis)


def shards(acts, grad_out, left_factor, right_factor, left_basis, right_basis, moment, second):
    width = grad_out.shape[1]
    blocks = left_factor.shape[0]
    groups = B // width
    nbits = groups.bit_length() - 1
    member = lax.axis_index("col") % groups
    contract = (((0,), (0,)), ((), ()))
    term = lax.dot_general(
        lax.all_gather(acts, "col", axis=1, tiled=True),
        grad_out,
        contract,
        preferred_element_type=jnp.float32,
    )
    grad = lax.psum_scatter(term, "tok", scatter_dimension=0, tiled=True)
    own = grad.astype(jnp.bfloat16).reshape(blocks, B, width)
    tiles, left_full, right_full = (own, left_basis, right_basis)
    for bit in range(nbits):
        other = swapped((tiles, left_full, right_full), "col", bit)
        lower = member >> bit & 1 == 0
        tiles = join_pair(tiles, other[0], 2, lower)
        left_full = join_pair(left_full, other[1], 1, lower)
        right_full = join_pair(right_full, other[2], 1, lower)
    right_cols = lax.dynamic_slice_in_dim(right_full, member * width, width, 2)
    mixed = jnp.einsum(
        "nab,nbc->nac", tiles, right_cols, preferred_element_type=jnp.float32
    ).astype(jnp.bfloat16)
    lead = lax.dynamic_slice_in_dim(tiles, member * width, width, 1)
    left_new = shampoo_beta * left_factor + (1.0 - shampoo_beta) * jnp.einsum(
        "nab,ncb->nac", lead, tiles, preferred_element_type=jnp.float32
    )
    right_new = shampoo_beta * right_factor + (1.0 - shampoo_beta) * jnp.einsum(
        "nat,nab->ntb", own, tiles, preferred_element_type=jnp.float32
    )
    rotated = jnp.einsum("nab,nac->nbc", left_full, mixed, preferred_element_type=jnp.float32)
    first_new = first_beta * moment.reshape(blocks, B, width) + (1.0 - first_beta) * rotated
    second_new = (
        second_beta * second.reshape(blocks, B, width) + (1.0 - second_beta) * rotated * rotated
    )
    normed = (first_new / first_corr / (jnp.sqrt(second_new / second_corr) + epsilon)).astype(
        jnp.bfloat16
    )
    steps_full = normed
    for bit in range(nbits):
        other_steps = swapped(steps_full, "col", bit)
        lower = member >> bit & 1 == 0
        steps_full = join_pair(steps_full, other_steps, 2, lower)
    back = jnp.einsum(
        "nab,ncb->nac", steps_full, right_basis, preferred_element_type=jnp.float32
    ).astype(jnp.bfloat16)
    update = jnp.einsum("nab,nbc->nac", left_full, back, preferred_element_type=jnp.float32).astype(
        jnp.bfloat16
    )
    rows = blocks * B
    return (
        left_new,
        right_new,
        first_new.reshape(rows, width),
        second_new.reshape(rows, width),
        update.reshape(rows, width),
    )


def solution(mesh):
    in_specs = (
        P("tok", "col"),
        P("tok", "col"),
        P("tok", "col", None),
        P("tok", "col", None),
        P("tok", "col", None),
        P("tok", "col", None),
        P("tok", "col"),
        P("tok", "col"),
    )
    out_specs = (
        P("tok", "col", None),
        P("tok", "col", None),
        P("tok", "col"),
        P("tok", "col"),
        P("tok", "col"),
    )
    return jax.shard_map(shards, mesh=mesh, in_specs=in_specs, out_specs=out_specs, check_vma=False)
```

profile of v0, /device:TPU:9, one launch (start us, length us, event | category | flops | bytes accessed | tf_op | source)
XLA Modules:
  0.0 488.8 jit_solution(3307319483804612024)
XLA Ops:
  7.2 0.0 copy-start
  7.2 0.0 all-gather.2.cloned.1.call-start
  7.2 0.7 all-gather.2.cloned.1.call-update
  7.9 0.0 reduce-scatter.2.cloned.1.call-start
  8.0 126.3 %all-gather.2.cloned.1.call-done = bf16[256,8192]{1,0:T(8,128)(2,1)} async-done(((bf16[256,128]{1,0:T(8,128)(2,1)}), bf16[256,8192]{1,0:T(8,128)(2,1)}) %all-gather.2.cloned.1.call-update) | async-done | bytes 4194320 | tf_op jit(solution)/shard_map/all_gather | solution.py:38
  134.3 0.0 copy-done
  134.3 5.4 %fusion.50 = f32[8192,128]{1,0:T(8,128)} fusion(bf16[256,8192]{1,0:T(8,128)(2,1)} %all-gather.2.cloned.1.call-done, bf16[256,128]{1,0:T(8,128)(2,1)S(1)} %copy-done), kind=kOutput, calls=%fused_computation.54 | convolution fusion | flops 536870912 | bytes 8454144 | tf_op jit(solution)/shard_map/dot_general | solution.py:37
  139.7 0.0 reduce-scatter.2.cloned.1.call-update
  139.7 0.9 copy-done.7
  140.7 1.9 collective-permute-start.6
  142.6 3.4 collective-permute-start.3
  146.0 0.1 broadcast.45.clone.1
  146.1 1.7 collective-permute-done.6
  147.8 2.3 collective-permute-start.7
  150.1 0.1 broadcast.45.clone
  150.2 2.5 collective-permute-done.3
  152.7 1.9 collective-permute-start.4
  154.6 44.9 %reduce-scatter.2.cloned.1.call-done = f32[1024,128]{1,0:T(8,128)} async-done(((f32[8192,128]{1,0:T(8,128)}), f32[1024,128]{1,0:T(8,128)}) %reduce-scatter.2.cloned.1.call-update) | async-done | bytes 524304 | tf_op jit(solution)/shard_map/reduce_scatter | solution.py:43
  199.6 0.8 broadcast.41.clone
  200.4 1.9 constant_dynamic-update-slice_fusion.19
  202.3 3.2 collective-permute-start
  205.6 0.1 broadcast.44.clone.1
  205.7 0.0 collective-permute-done.7
  205.8 6.8 %collective-permute-start.8 = (bf16[1,512,1024]{2,1,0:T(8,128)(2,1)S(1)}, bf16[1,512,1024]{2,1,0:T(8,128)(2,1)}, u32[]{:S(2)}, u32[]{:S(2)}) collective-permute-start(bf16[1,512,1024]{2,1,0:T(8,128)(2,1)S(1)} %constant_dynamic-update-slice_fusion.6), channel_id=1, source_target_pairs={{0,32},{8,40},{16,48},{24,56},{32,0},{40,8},{48,16},{56,24},{64,96... | collective-permute-start | bytes 3145736 | tf_op jit(solution)/shard_map/ppermute | solution.py:16
  212.7 0.0 collective-permute-done
  212.7 1.7 constant_dynamic-update-slice_fusion.18
  214.3 3.4 collective-permute-start.1
  217.8 0.1 broadcast.44.clone
  218.0 0.0 collective-permute-done.4
  218.0 7.8 %collective-permute-start.5 = (bf16[1,512,1024]{2,1,0:T(8,128)(2,1)S(1)}, bf16[1,512,1024]{2,1,0:T(8,128)(2,1)}, u32[]{:S(2)}, u32[]{:S(2)}) collective-permute-start(bf16[1,512,1024]{2,1,0:T(8,128)(2,1)S(1)} %constant_dynamic-update-slice_fusion.10), channel_id=1, source_target_pairs={{0,32},{8,40},{16,48},{24,56},{32,0},{40,8},{48,16},{56,24},{64,96... | collective-permute-start | bytes 3145736 | tf_op jit(solution)/shard_map/ppermute | solution.py:16
  225.8 0.1 broadcast.40.clone
  225.9 1.1 constant_dynamic-update-slice_fusion.17
  227.0 100.2 %collective-permute-done.1 = bf16[1,1024,256]{2,1,0:T(8,128)(2,1)S(1)} collective-permute-done((bf16[1,1024,256]{2,1,0:T(8,128)(2,1)}, bf16[1,1024,256]{2,1,0:T(8,128)(2,1)S(1)}, u32[]{:S(2)}, u32[]{:S(2)}) %collective-permute-start.1) | collective-permute-done | bytes 524320 | tf_op jit(solution)/shard_map/ppermute | solution.py:16
  327.2 5.2 %collective-permute-start.2 = (bf16[1,1024,512]{2,1,0:T(8,128)(2,1)S(1)}, bf16[1,1024,512]{2,1,0:T(8,128)(2,1)}, u32[]{:S(2)}, u32[]{:S(2)}) collective-permute-start(bf16[1,1024,512]{2,1,0:T(8,128)(2,1)S(1)} %constant_dynamic-update-slice_fusion.16), channel_id=1, source_target_pairs={{0,32},{8,40},{16,48},{24,56},{32,0},{40,8},{48,16},{56,24},{64,96... | collective-permute-start | bytes 3145736 | tf_op jit(solution)/shard_map/ppermute | solution.py:16
  332.4 0.3 broadcast.39.clone.1
  332.6 0.1 constant_dynamic-update-slice_fusion.5
  332.8 0.3 broadcast.43.clone
  333.0 0.1 bitcast_dynamic-update-slice_fusion.3
  333.1 0.0 collective-permute-done.8
  333.2 1.3 constant_dynamic-update-slice_fusion.4
  334.5 0.0 collective-permute-done.5
  334.5 2.1 bitcast_dynamic-update-slice_fusion.2
  336.6 0.3 broadcast.39.clone
  336.9 0.2 constant_dynamic-update-slice_fusion.15
  337.1 0.9 copy-done.2
  337.9 42.3 %collective-permute-done.2 = bf16[1,1024,512]{2,1,0:T(8,128)(2,1)} collective-permute-done((bf16[1,1024,512]{2,1,0:T(8,128)(2,1)S(1)}, bf16[1,1024,512]{2,1,0:T(8,128)(2,1)}, u32[]{:S(2)}, u32[]{:S(2)}) %collective-permute-start.2) | collective-permute-done | bytes 1048608 | tf_op jit(solution)/shard_map/ppermute | solution.py:16
  380.3 1.4 constant_dynamic-update-slice_fusion.14
  381.7 5.3 %constant_dynamic-update-slice_fusion.3 = (bf16[1,1024,256]{2,1,0:T(8,128)(2,1)S(1)}, bf16[1,1024,128]{2,1,0:T(8,128)(2,1)S(1)}, f32[1024,128]{1,0:T(8,128)}, f32[1024,128]{1,0:T(8,128)}) fusion(bf16[1,1024,256]{2,1,0:T(8,128)(2,1)S(1)} %broadcast.41, s32[]{:T(128)S(6)} %select_n.61, f32[1024,128]{1,0:T(8,128)} %param.15, f32[1024,128]{1,0:T(8,128)} %param.14, ...), kind=kOutput, calls=%fused_computation.35 | convolution fusion | flops 538574848 | bytes 7077896 | tf_op jit(solution)/shard_map/nab,nac->nbc/dot_general | solution.py:63
  387.1 2.0 collective-permute-start.9
  389.1 7.0 %collective-permute-done.9 = bf16[1,1024,128]{2,1,0:T(8,128)(2,1)S(1)} collective-permute-done((bf16[1,1024,128]{2,1,0:T(8,128)(2,1)S(1)}, bf16[1,1024,128]{2,1,0:T(8,128)(2,1)S(1)}, u32[]{:S(2)}, u32[]{:S(2)}) %collective-permute-start.9) | collective-permute-done | bytes 262176 | tf_op jit(solution)/shard_map/ppermute | solution.py:16
  396.1 0.1 constant_dynamic-update-slice_fusion.2
  396.1 2.8 collective-permute-start.10
  399.0 0.1 broadcast.40
  399.1 0.0 copy-start.4
  399.1 24.9 %collective-permute-done.10 = bf16[1,1024,256]{2,1,0:T(8,128)(2,1)S(1)} collective-permute-done((bf16[1,1024,256]{2,1,0:T(8,128)(2,1)S(1)}, bf16[1,1024,256]{2,1,0:T(8,128)(2,1)S(1)}, u32[]{:S(2)}, u32[]{:S(2)}) %collective-permute-start.10) | collective-permute-done | bytes 524320 | tf_op jit(solution)/shard_map/ppermute | solution.py:16
  424.0 5.1 %collective-permute-start.11 = (bf16[1,1024,512]{2,1,0:T(8,128)(2,1)S(1)}, bf16[1,1024,512]{2,1,0:T(8,128)(2,1)S(1)}, u32[]{:S(2)}, u32[]{:S(2)}) collective-permute-start(bf16[1,1024,512]{2,1,0:T(8,128)(2,1)S(1)} %constant_dynamic-update-slice_fusion), channel_id=1, source_target_pairs={{0,32},{8,40},{16,48},{24,56},{32,0},{40,8},{48,16},{56,24},{64,96... | collective-permute-start | bytes 3145736 | tf_op jit(solution)/shard_map/ppermute | solution.py:16
  429.2 1.6 fusion.21
  430.8 0.0 copy-done.3
  430.8 1.3 fusion.18
  432.1 0.3 broadcast.43
  432.3 0.1 bitcast_dynamic-update-slice_fusion.1
  432.5 44.8 %collective-permute-done.11 = bf16[1,1024,512]{2,1,0:T(8,128)(2,1)S(1)} collective-permute-done((bf16[1,1024,512]{2,1,0:T(8,128)(2,1)S(1)}, bf16[1,1024,512]{2,1,0:T(8,128)(2,1)S(1)}, u32[]{:S(2)}, u32[]{:S(2)}) %collective-permute-start.11) | collective-permute-done | bytes 1048608 | tf_op jit(solution)/shard_map/ppermute | solution.py:16
  477.3 0.1 bitcast_dynamic-update-slice_fusion
  477.5 4.5 convolution_convert_fusion
  (22 shorter events, 0.5 us)
Async XLA Ops:
  7.2 127.1 %copy-start = (bf16[256,128]{1,0:T(8,128)(2,1)S(1)}, bf16[256,128]{1,0:T(8,128)(2,1)}, u32[]{:S(2)}) copy-start(bf16[256,128]{1,0:T(8,128)(2,1)} %param.9) | copy-start | bytes 196612
  7.2 127.1 %all-gather.2.cloned.1.call-start = ((), (), s32[]{:S(2)}) async-start(), calls=%async_computation.1 | async-start | bytes 4259840 | tf_op jit(solution)/shard_map/all_gather | solution.py:38
  7.9 191.7 %reduce-scatter.2.cloned.1.call-start = ((), (), s32[]{:S(2)}) async-start(), calls=%async_computation.2 | async-start | bytes 4718592 | tf_op jit(solution)/shard_map/reduce_scatter | solution.py:43
  139.7 0.9 copy-start.7
  139.7 2.9 copy-start.6
  140.7 7.1 %collective-permute-start.6 = (bf16[1,128,1024]{2,1,0:T(8,128)(2,1)S(1)}, bf16[1,128,1024]{2,1,0:T(8,128)(2,1)S(1)}, u32[]{:S(2)}, u32[]{:S(2)}) collective-permute-start(bf16[1,128,1024]{2,1,0:T(8,128)(2,1)S(1)} %copy-done.7), channel_id=1, source_target_pairs={{0,8},{8,0},{16,24},{24,16},{32,40},{40,32},{48,56},{56,48},{64,72... | collective-permute-start | bytes 786440 | tf_op jit(solution)/shard_map/ppermute | solution.py:16
  142.6 10.1 %collective-permute-start.3 = (bf16[1,128,1024]{2,1,0:T(8,128)(2,1)S(1)}, bf16[1,128,1024]{2,1,0:T(8,128)(2,1)S(1)}, u32[]{:S(2)}, u32[]{:S(2)}) collective-permute-start(bf16[1,128,1024]{2,1,0:T(8,128)(2,1)S(1)} %copy-done.6), channel_id=1, source_target_pairs={{0,8},{8,0},{16,24},{24,16},{32,40},{40,32},{48,56},{56,48},{64,72... | collective-permute-start | bytes 786440 | tf_op jit(solution)/shard_map/ppermute | solution.py:16
  147.8 58.0 %collective-permute-start.7 = (bf16[1,256,1024]{2,1,0:T(8,128)(2,1)S(1)}, bf16[1,256,1024]{2,1,0:T(8,128)(2,1)S(1)}, u32[]{:S(2)}, u32[]{:S(2)}) collective-permute-start(bf16[1,256,1024]{2,1,0:T(8,128)(2,1)S(1)} %constant_dynamic-update-slice_fusion.8), channel_id=1, source_target_pairs={{0,16},{8,24},{16,0},{24,8},{32,48},{40,56},{48,32},{56,40},{64,80... | collective-permute-start | bytes 1572872 | tf_op jit(solution)/shard_map/ppermute | solution.py:16
  152.7 65.3 %collective-permute-start.4 = (bf16[1,256,1024]{2,1,0:T(8,128)(2,1)S(1)}, bf16[1,256,1024]{2,1,0:T(8,128)(2,1)S(1)}, u32[]{:S(2)}, u32[]{:S(2)}) collective-permute-start(bf16[1,256,1024]{2,1,0:T(8,128)(2,1)S(1)} %constant_dynamic-update-slice_fusion.12), channel_id=1, source_target_pairs={{0,16},{8,24},{16,0},{24,8},{32,48},{40,56},{48,32},{56,40},{64,80... | collective-permute-start | bytes 1572872 | tf_op jit(solution)/shard_map/ppermute | solution.py:16
  202.3 10.4 %collective-permute-start = (bf16[1,1024,128]{2,1,0:T(8,128)(2,1)}, bf16[1,1024,128]{2,1,0:T(8,128)(2,1)}, u32[]{:S(2)}, u32[]{:S(2)}) collective-permute-start(bf16[1,1024,128]{2,1,0:T(8,128)(2,1)} %get-tuple-element.10), channel_id=1, source_target_pairs={{0,8},{8,0},{16,24},{24,16},{32,40},{40,32},{48,56},{56,48},{64,72... | collective-permute-start | bytes 786440 | tf_op jit(solution)/shard_map/ppermute | solution.py:16
  205.8 127.3 %collective-permute-start.8 = (bf16[1,512,1024]{2,1,0:T(8,128)(2,1)S(1)}, bf16[1,512,1024]{2,1,0:T(8,128)(2,1)}, u32[]{:S(2)}, u32[]{:S(2)}) collective-permute-start(bf16[1,512,1024]{2,1,0:T(8,128)(2,1)S(1)} %constant_dynamic-update-slice_fusion.6), channel_id=1, source_target_pairs={{0,32},{8,40},{16,48},{24,56},{32,0},{40,8},{48,16},{56,24},{64,96... | collective-permute-start | bytes 3145736 | tf_op jit(solution)/shard_map/ppermute | solution.py:16
  214.3 112.8 %collective-permute-start.1 = (bf16[1,1024,256]{2,1,0:T(8,128)(2,1)}, bf16[1,1024,256]{2,1,0:T(8,128)(2,1)S(1)}, u32[]{:S(2)}, u32[]{:S(2)}) collective-permute-start(bf16[1,1024,256]{2,1,0:T(8,128)(2,1)} %constant_dynamic-update-slice_fusion.18), channel_id=1, source_target_pairs={{0,16},{8,24},{16,0},{24,8},{32,48},{40,56},{48,32},{56,40},{64,80... | collective-permute-start | bytes 1572872 | tf_op jit(solution)/shard_map/ppermute | solution.py:16
  218.0 116.5 %collective-permute-start.5 = (bf16[1,512,1024]{2,1,0:T(8,128)(2,1)S(1)}, bf16[1,512,1024]{2,1,0:T(8,128)(2,1)}, u32[]{:S(2)}, u32[]{:S(2)}) collective-permute-start(bf16[1,512,1024]{2,1,0:T(8,128)(2,1)S(1)} %constant_dynamic-update-slice_fusion.10), channel_id=1, source_target_pairs={{0,32},{8,40},{16,48},{24,56},{32,0},{40,8},{48,16},{56,24},{64,96... | collective-permute-start | bytes 3145736 | tf_op jit(solution)/shard_map/ppermute | solution.py:16
  327.2 53.1 %collective-permute-start.2 = (bf16[1,1024,512]{2,1,0:T(8,128)(2,1)S(1)}, bf16[1,1024,512]{2,1,0:T(8,128)(2,1)}, u32[]{:S(2)}, u32[]{:S(2)}) collective-permute-start(bf16[1,1024,512]{2,1,0:T(8,128)(2,1)S(1)} %constant_dynamic-update-slice_fusion.16), channel_id=1, source_target_pairs={{0,32},{8,40},{16,48},{24,56},{32,0},{40,8},{48,16},{56,24},{64,96... | collective-permute-start | bytes 3145736 | tf_op jit(solution)/shard_map/ppermute | solution.py:16
  334.5 2.4 copy-start.1
  336.6 1.3 copy-start.2
  387.1 42.1 %copy-start.5 = (f32[1,128,1024]{2,1,0:T(8,128)S(1)}, f32[1,128,1024]{2,1,0:T(8,128)}, u32[]{:S(2)}) copy-start(f32[1,128,1024]{2,1,0:T(8,128)} %param.10) | copy-start | bytes 1572868
  387.1 9.0 %collective-permute-start.9 = (bf16[1,1024,128]{2,1,0:T(8,128)(2,1)S(1)}, bf16[1,1024,128]{2,1,0:T(8,128)(2,1)S(1)}, u32[]{:S(2)}, u32[]{:S(2)}) collective-permute-start(bf16[1,1024,128]{2,1,0:T(8,128)(2,1)S(1)} %get-tuple-element.6), channel_id=1, source_target_pairs={{0,8},{8,0},{16,24},{24,16},{32,40},{40,32},{48,56},{56,48},{64,72... | collective-permute-start | bytes 786440 | tf_op jit(solution)/shard_map/ppermute | solution.py:16
  396.1 27.9 %collective-permute-start.10 = (bf16[1,1024,256]{2,1,0:T(8,128)(2,1)S(1)}, bf16[1,1024,256]{2,1,0:T(8,128)(2,1)S(1)}, u32[]{:S(2)}, u32[]{:S(2)}) collective-permute-start(bf16[1,1024,256]{2,1,0:T(8,128)(2,1)S(1)} %constant_dynamic-update-slice_fusion.2), channel_id=1, source_target_pairs={{0,16},{8,24},{16,0},{24,8},{32,48},{40,56},{48,32},{56,40},{64,80... | collective-permute-start | bytes 1572872 | tf_op jit(solution)/shard_map/ppermute | solution.py:16
  399.1 31.7 %copy-start.3 = (f32[1024,128]{1,0:T(8,128)S(1)}, f32[1024,128]{1,0:T(8,128)}, u32[]{:S(2)}) copy-start(f32[1024,128]{1,0:T(8,128)} %reduce-scatter.2.cloned.1.call-done) | copy-start | bytes 1572868
  399.1 31.7 %copy-start.4 = (f32[1,128,1024]{2,1,0:T(8,128)S(1)}, f32[1,128,1024]{2,1,0:T(8,128)}, u32[]{:S(2)}) copy-start(f32[1,128,1024]{2,1,0:T(8,128)} %param.11) | copy-start | bytes 1572868
  424.0 53.3 %collective-permute-start.11 = (bf16[1,1024,512]{2,1,0:T(8,128)(2,1)S(1)}, bf16[1,1024,512]{2,1,0:T(8,128)(2,1)S(1)}, u32[]{:S(2)}, u32[]{:S(2)}) collective-permute-start(bf16[1,1024,512]{2,1,0:T(8,128)(2,1)S(1)} %constant_dynamic-update-slice_fusion), channel_id=1, source_target_pairs={{0,32},{8,40},{16,48},{24,56},{32,0},{40,8},{48,16},{56,24},{64,96... | collective-permute-start | bytes 3145736 | tf_op jit(solution)/shard_map/ppermute | solution.py:16
Sparse Core Ops, SparseCore 0:
  12.3 121.9 all-gather.1
  139.9 59.6 reduce-scatter.1
where the time goes:
time: 490 us; the launch traced here: 489 us
  waiting for transfers between devices  395 us (81%)
  starting transfers between devices  46 us (9%)
  matrix products  18.2 us (4%)
  between operations  14.5 us (3%)
  local copies, waits for them, and re-layouts  12.9 us (3%)
    ppermute x12, waiting for transfers between devices, swapped(): lax.ppermute(array, axis, [(i, i ^ 1 << distance) for i in range(lax.axis...  223 us
    all_gather x1, waiting for transfers between devices, shards(): lax.all_gather(acts, 'col', axis=1, tiled=True)  126 us
    ppermute x12, starting transfers between devices, swapped(): lax.ppermute(array, axis, [(i, i ^ 1 << distance) for i in range(lax.axis...  45.9 us
    reduce_scatter x1, waiting for transfers between devices, shards(): grad = lax.psum_scatter(term, 'tok', scatter_dimension=0, tiled=True)  44.9 us
  transfers between devices with their start and end apart: 14, of which 9 were waited for; matrix products, arithmetic and copies ran while one was open for 3% of the time, Pallas kernels for 0%

commit v1 on v0

--- a/solution.py
+++ b/solution.py
@@ -35,7 +35,9 @@
     member = lax.axis_index("col") % groups
     contract = (((0,), (0,)), ((), ()))
     term = lax.dot_general(
-        lax.all_gather(acts, "col", axis=1, tiled=True),
+        jnp.concatenate(
+            lax.all_to_all(jnp.stack([acts] * lax.axis_size("col")), "col", 0, 0), axis=1
+        ),
         grad_out,
         contract,
         preferred_element_type=jnp.float32,

time: 490 us -> 480 us (0.980)
  the two profiles are of different devices: /device:TPU:9 before, /device:TPU:11 now
where the time goes in v1:
time: 480 us; the launch traced here: 479 us
  waiting for transfers between devices  261 us (54%)
  blocking collectives  122 us (25%)
  starting transfers between devices  48.5 us (10%)
  matrix products  16 us (3%)
  between operations  14.5 us (3%)
  local copies, waits for them, and re-layouts  14.3 us (3%)
    ppermute x12, waiting for transfers between devices, swapped(): lax.ppermute(array, axis, [(i, i ^ 1 << distance) for i in range(lax.axis...  223 us
    all_to_all x1, blocking collectives, shards(): lax.all_to_all(jnp.stack([acts] * lax.axis_size('col')), 'col', 0, 0)  122 us
    ppermute x12, starting transfers between devices, swapped(): lax.ppermute(array, axis, [(i, i ^ 1 << distance) for i in range(lax.axis...  48.4 us
    reduce_scatter x1, waiting for transfers between devices, shards(): grad = lax.psum_scatter(term, 'tok', scatter_dimension=0, tiled=True)  38.1 us
  transfers between devices with their start and end apart: 13, of which 8 were waited for; matrix products, arithmetic and copies ran while one was open for 3% of the time, Pallas kernels for 0%

profile of v1, /device:TPU:11, one launch (start us, length us, event | category | flops | bytes accessed | tf_op | source)
XLA Modules:
  0.0 478.9 jit_solution(14204031253762432484)
XLA Ops:
  7.2 0.0 copy-start
  7.2 0.0 reduce-scatter.2.cloned.1.call-start
  7.2 0.9 copy.13
  8.2 0.5 stack.2
  8.7 122.2 %all_to_all.5 = bf16[64,256,128]{1,2,0:T(8,128)(2,1)S(1)} all-to-all(bf16[64,256,128]{1,2,0:T(8,128)(2,1)S(1)} %stack.2), channel_id=1, replica_groups=mesh['col'=64,'tok'=8] {'col'}, dimensions={0} | all-to-all | bytes 8388608 | tf_op jit(solution)/shard_map/all_to_all | solution.py:39
  130.9 0.0 copy-done
  130.9 3.2 fusion.50
  134.1 0.0 reduce-scatter.2.cloned.1.call-update
  134.1 0.9 copy-done.7
  135.1 3.3 collective-permute-start.6
  138.4 0.0 copy-done.6
  138.4 1.9 collective-permute-start.3
  140.4 0.1 broadcast.47.clone.1
  140.5 3.0 collective-permute-done.6
  143.5 2.5 collective-permute-start.7
  146.0 0.1 broadcast.47.clone
  146.1 3.1 collective-permute-done.3
  149.2 2.4 collective-permute-start.4
  151.6 38.1 %reduce-scatter.2.cloned.1.call-done = f32[1024,128]{1,0:T(8,128)} async-done(((f32[8192,128]{1,0:T(8,128)}), f32[1024,128]{1,0:T(8,128)}) %reduce-scatter.2.cloned.1.call-update) | async-done | bytes 524304 | tf_op jit(solution)/shard_map/reduce_scatter | solution.py:45
  189.8 0.8 broadcast.43.clone
  190.6 1.9 constant_dynamic-update-slice_fusion.19
  192.5 3.1 collective-permute-start
  195.6 0.1 broadcast.46.clone.1
  195.8 0.0 collective-permute-done.7
  195.8 6.8 %collective-permute-start.8 = (bf16[1,512,1024]{2,1,0:T(8,128)(2,1)S(1)}, bf16[1,512,1024]{2,1,0:T(8,128)(2,1)}, u32[]{:S(2)}, u32[]{:S(2)}) collective-permute-start(bf16[1,512,1024]{2,1,0:T(8,128)(2,1)S(1)} %constant_dynamic-update-slice_fusion.6), channel_id=1, source_target_pairs={{0,32},{8,40},{16,48},{24,56},{32,0},{40,8},{48,16},{56,24},{64,96... | collective-permute-start | bytes 3145736 | tf_op jit(solution)/shard_map/ppermute | solution.py:16
  202.7 0.0 collective-permute-done
  202.7 1.7 constant_dynamic-update-slice_fusion.18
  204.3 3.5 collective-permute-start.1
  207.8 0.1 broadcast.46.clone
  208.0 0.0 collective-permute-done.4
  208.1 9.8 %collective-permute-start.5 = (bf16[1,512,1024]{2,1,0:T(8,128)(2,1)S(1)}, bf16[1,512,1024]{2,1,0:T(8,128)(2,1)}, u32[]{:S(2)}, u32[]{:S(2)}) collective-permute-start(bf16[1,512,1024]{2,1,0:T(8,128)(2,1)S(1)} %constant_dynamic-update-slice_fusion.10), channel_id=1, source_target_pairs={{0,32},{8,40},{16,48},{24,56},{32,0},{40,8},{48,16},{56,24},{64,96... | collective-permute-start | bytes 3145736 | tf_op jit(solution)/shard_map/ppermute | solution.py:16
  217.9 0.1 broadcast.42.clone
  217.9 1.1 constant_dynamic-update-slice_fusion.17
  219.0 98.1 %collective-permute-done.1 = bf16[1,1024,256]{2,1,0:T(8,128)(2,1)S(1)} collective-permute-done((bf16[1,1024,256]{2,1,0:T(8,128)(2,1)}, bf16[1,1024,256]{2,1,0:T(8,128)(2,1)S(1)}, u32[]{:S(2)}, u32[]{:S(2)}) %collective-permute-start.1) | collective-permute-done | bytes 524320 | tf_op jit(solution)/shard_map/ppermute | solution.py:16
  317.2 5.2 %collective-permute-start.2 = (bf16[1,1024,512]{2,1,0:T(8,128)(2,1)S(1)}, bf16[1,1024,512]{2,1,0:T(8,128)(2,1)}, u32[]{:S(2)}, u32[]{:S(2)}) collective-permute-start(bf16[1,1024,512]{2,1,0:T(8,128)(2,1)S(1)} %constant_dynamic-update-slice_fusion.16), channel_id=1, source_target_pairs={{0,32},{8,40},{16,48},{24,56},{32,0},{40,8},{48,16},{56,24},{64,96... | collective-permute-start | bytes 3145736 | tf_op jit(solution)/shard_map/ppermute | solution.py:16
  322.4 0.3 broadcast.41.clone.1
  322.7 0.1 constant_dynamic-update-slice_fusion.5
  322.8 0.3 broadcast.45.clone
  323.0 0.1 bitcast_dynamic-update-slice_fusion.3
  323.2 0.0 collective-permute-done.8
  323.2 1.3 constant_dynamic-update-slice_fusion.4
  324.5 0.0 collective-permute-done.5
  324.5 2.1 bitcast_dynamic-update-slice_fusion.2
  326.6 0.3 broadcast.41.clone
  326.9 0.2 constant_dynamic-update-slice_fusion.15
  327.1 0.9 copy-done.2
  328.0 42.4 %collective-permute-done.2 = bf16[1,1024,512]{2,1,0:T(8,128)(2,1)} collective-permute-done((bf16[1,1024,512]{2,1,0:T(8,128)(2,1)S(1)}, bf16[1,1024,512]{2,1,0:T(8,128)(2,1)}, u32[]{:S(2)}, u32[]{:S(2)}) %collective-permute-start.2) | collective-permute-done | bytes 1048608 | tf_op jit(solution)/shard_map/ppermute | solution.py:16
  370.3 1.4 constant_dynamic-update-slice_fusion.14
  371.8 5.3 %constant_dynamic-update-slice_fusion.3 = (bf16[1,1024,256]{2,1,0:T(8,128)(2,1)S(1)}, bf16[1,1024,128]{2,1,0:T(8,128)(2,1)S(1)}, f32[1024,128]{1,0:T(8,128)}, f32[1024,128]{1,0:T(8,128)}) fusion(bf16[1,1024,256]{2,1,0:T(8,128)(2,1)S(1)} %broadcast.43, s32[]{:T(128)S(6)} %select_n.61, f32[1024,128]{1,0:T(8,128)} %param.15, f32[1024,128]{1,0:T(8,128)} %param.14, ...), kind=kOutput, calls=%fused_computation.35 | convolution fusion | flops 538574848 | bytes 7077896 | tf_op jit(solution)/shard_map/nab,nac->nbc/dot_general | solution.py:65
  377.1 2.0 collective-permute-start.9
  379.1 7.0 %collective-permute-done.9 = bf16[1,1024,128]{2,1,0:T(8,128)(2,1)S(1)} collective-permute-done((bf16[1,1024,128]{2,1,0:T(8,128)(2,1)S(1)}, bf16[1,1024,128]{2,1,0:T(8,128)(2,1)S(1)}, u32[]{:S(2)}, u32[]{:S(2)}) %collective-permute-start.9) | collective-permute-done | bytes 262176 | tf_op jit(solution)/shard_map/ppermute | solution.py:16
  386.1 0.1 constant_dynamic-update-slice_fusion.2
  386.2 2.8 collective-permute-start.10
  389.0 0.1 broadcast.42
  389.1 0.0 copy-start.4
  389.1 24.9 %collective-permute-done.10 = bf16[1,1024,256]{2,1,0:T(8,128)(2,1)S(1)} collective-permute-done((bf16[1,1024,256]{2,1,0:T(8,128)(2,1)S(1)}, bf16[1,1024,256]{2,1,0:T(8,128)(2,1)S(1)}, u32[]{:S(2)}, u32[]{:S(2)}) %collective-permute-start.10) | collective-permute-done | bytes 524320 | tf_op jit(solution)/shard_map/ppermute | solution.py:16
  414.1 5.1 %collective-permute-start.11 = (bf16[1,1024,512]{2,1,0:T(8,128)(2,1)S(1)}, bf16[1,1024,512]{2,1,0:T(8,128)(2,1)S(1)}, u32[]{:S(2)}, u32[]{:S(2)}) collective-permute-start(bf16[1,1024,512]{2,1,0:T(8,128)(2,1)S(1)} %constant_dynamic-update-slice_fusion), channel_id=1, source_target_pairs={{0,32},{8,40},{16,48},{24,56},{32,0},{40,8},{48,16},{56,24},{64,96... | collective-permute-start | bytes 3145736 | tf_op jit(solution)/shard_map/ppermute | solution.py:16
  419.2 1.6 fusion.21
  420.8 1.3 fusion.18
  422.1 0.3 broadcast.45
  422.4 0.1 bitcast_dynamic-update-slice_fusion.1
  422.5 44.9 %collective-permute-done.11 = bf16[1,1024,512]{2,1,0:T(8,128)(2,1)S(1)} collective-permute-done((bf16[1,1024,512]{2,1,0:T(8,128)(2,1)S(1)}, bf16[1,1024,512]{2,1,0:T(8,128)(2,1)S(1)}, u32[]{:S(2)}, u32[]{:S(2)}) %collective-permute-start.11) | collective-permute-done | bytes 1048608 | tf_op jit(solution)/shard_map/ppermute | solution.py:16
  467.4 0.1 bitcast_dynamic-update-slice_fusion
  467.5 4.5 convolution_convert_fusion
  (22 shorter events, 0.5 us)
Async XLA Ops:
  7.2 123.7 %copy-start = (bf16[256,128]{1,0:T(8,128)(2,1)S(1)}, bf16[256,128]{1,0:T(8,128)(2,1)}, u32[]{:S(2)}) copy-start(bf16[256,128]{1,0:T(8,128)(2,1)} %param.9) | copy-start | bytes 196612
  7.2 182.6 %reduce-scatter.2.cloned.1.call-start = ((), (), s32[]{:S(2)}) async-start(), calls=%async_computation.2 | async-start | bytes 4718592 | tf_op jit(solution)/shard_map/reduce_scatter | solution.py:45
  134.1 0.9 copy-start.7
  134.1 4.3 copy-start.6
  135.1 8.4 %collective-permute-start.6 = (bf16[1,128,1024]{2,1,0:T(8,128)(2,1)S(1)}, bf16[1,128,1024]{2,1,0:T(8,128)(2,1)S(1)}, u32[]{:S(2)}, u32[]{:S(2)}) collective-permute-start(bf16[1,128,1024]{2,1,0:T(8,128)(2,1)S(1)} %copy-done.7), channel_id=1, source_target_pairs={{0,8},{8,0},{16,24},{24,16},{32,40},{40,32},{48,56},{56,48},{64,72... | collective-permute-start | bytes 786440 | tf_op jit(solution)/shard_map/ppermute | solution.py:16
  138.4 10.8 %collective-permute-start.3 = (bf16[1,128,1024]{2,1,0:T(8,128)(2,1)S(1)}, bf16[1,128,1024]{2,1,0:T(8,128)(2,1)S(1)}, u32[]{:S(2)}, u32[]{:S(2)}) collective-permute-start(bf16[1,128,1024]{2,1,0:T(8,128)(2,1)S(1)} %copy-done.6), channel_id=1, source_target_pairs={{0,8},{8,0},{16,24},{24,16},{32,40},{40,32},{48,56},{56,48},{64,72... | collective-permute-start | bytes 786440 | tf_op jit(solution)/shard_map/ppermute | solution.py:16
  143.5 52.3 %collective-permute-start.7 = (bf16[1,256,1024]{2,1,0:T(8,128)(2,1)S(1)}, bf16[1,256,1024]{2,1,0:T(8,128)(2,1)S(1)}, u32[]{:S(2)}, u32[]{:S(2)}) collective-permute-start(bf16[1,256,1024]{2,1,0:T(8,128)(2,1)S(1)} %constant_dynamic-update-slice_fusion.8), channel_id=1, source_target_pairs={{0,16},{8,24},{16,0},{24,8},{32,48},{40,56},{48,32},{56,40},{64,80... | collective-permute-start | bytes 1572872 | tf_op jit(solution)/shard_map/ppermute | solution.py:16
  149.2 58.8 %collective-permute-start.4 = (bf16[1,256,1024]{2,1,0:T(8,128)(2,1)S(1)}, bf16[1,256,1024]{2,1,0:T(8,128)(2,1)S(1)}, u32[]{:S(2)}, u32[]{:S(2)}) collective-permute-start(bf16[1,256,1024]{2,1,0:T(8,128)(2,1)S(1)} %constant_dynamic-update-slice_fusion.12), channel_id=1, source_target_pairs={{0,16},{8,24},{16,0},{24,8},{32,48},{40,56},{48,32},{56,40},{64,80... | collective-permute-start | bytes 1572872 | tf_op jit(solution)/shard_map/ppermute | solution.py:16
  192.5 10.2 %collective-permute-start = (bf16[1,1024,128]{2,1,0:T(8,128)(2,1)}, bf16[1,1024,128]{2,1,0:T(8,128)(2,1)}, u32[]{:S(2)}, u32[]{:S(2)}) collective-permute-start(bf16[1,1024,128]{2,1,0:T(8,128)(2,1)} %get-tuple-element.10), channel_id=1, source_target_pairs={{0,8},{8,0},{16,24},{24,16},{32,40},{40,32},{48,56},{56,48},{64,72... | collective-permute-start | bytes 786440 | tf_op jit(solution)/shard_map/ppermute | solution.py:16
  195.8 127.3 %collective-permute-start.8 = (bf16[1,512,1024]{2,1,0:T(8,128)(2,1)S(1)}, bf16[1,512,1024]{2,1,0:T(8,128)(2,1)}, u32[]{:S(2)}, u32[]{:S(2)}) collective-permute-start(bf16[1,512,1024]{2,1,0:T(8,128)(2,1)S(1)} %constant_dynamic-update-slice_fusion.6), channel_id=1, source_target_pairs={{0,32},{8,40},{16,48},{24,56},{32,0},{40,8},{48,16},{56,24},{64,96... | collective-permute-start | bytes 3145736 | tf_op jit(solution)/shard_map/ppermute | solution.py:16
  204.3 112.8 %collective-permute-start.1 = (bf16[1,1024,256]{2,1,0:T(8,128)(2,1)}, bf16[1,1024,256]{2,1,0:T(8,128)(2,1)S(1)}, u32[]{:S(2)}, u32[]{:S(2)}) collective-permute-start(bf16[1,1024,256]{2,1,0:T(8,128)(2,1)} %constant_dynamic-update-slice_fusion.18), channel_id=1, source_target_pairs={{0,16},{8,24},{16,0},{24,8},{32,48},{40,56},{48,32},{56,40},{64,80... | collective-permute-start | bytes 1572872 | tf_op jit(solution)/shard_map/ppermute | solution.py:16
  208.1 116.5 %collective-permute-start.5 = (bf16[1,512,1024]{2,1,0:T(8,128)(2,1)S(1)}, bf16[1,512,1024]{2,1,0:T(8,128)(2,1)}, u32[]{:S(2)}, u32[]{:S(2)}) collective-permute-start(bf16[1,512,1024]{2,1,0:T(8,128)(2,1)S(1)} %constant_dynamic-update-slice_fusion.10), channel_id=1, source_target_pairs={{0,32},{8,40},{16,48},{24,56},{32,0},{40,8},{48,16},{56,24},{64,96... | collective-permute-start | bytes 3145736 | tf_op jit(solution)/shard_map/ppermute | solution.py:16
  317.2 53.1 %collective-permute-start.2 = (bf16[1,1024,512]{2,1,0:T(8,128)(2,1)S(1)}, bf16[1,1024,512]{2,1,0:T(8,128)(2,1)}, u32[]{:S(2)}, u32[]{:S(2)}) collective-permute-start(bf16[1,1024,512]{2,1,0:T(8,128)(2,1)S(1)} %constant_dynamic-update-slice_fusion.16), channel_id=1, source_target_pairs={{0,32},{8,40},{16,48},{24,56},{32,0},{40,8},{48,16},{56,24},{64,96... | collective-permute-start | bytes 3145736 | tf_op jit(solution)/shard_map/ppermute | solution.py:16
  324.5 2.4 copy-start.1
  326.6 1.3 copy-start.2
  377.1 42.1 %copy-start.5 = (f32[1,128,1024]{2,1,0:T(8,128)S(1)}, f32[1,128,1024]{2,1,0:T(8,128)}, u32[]{:S(2)}) copy-start(f32[1,128,1024]{2,1,0:T(8,128)} %param.10) | copy-start | bytes 1572868
  377.1 9.0 %collective-permute-start.9 = (bf16[1,1024,128]{2,1,0:T(8,128)(2,1)S(1)}, bf16[1,1024,128]{2,1,0:T(8,128)(2,1)S(1)}, u32[]{:S(2)}, u32[]{:S(2)}) collective-permute-start(bf16[1,1024,128]{2,1,0:T(8,128)(2,1)S(1)} %get-tuple-element.6), channel_id=1, source_target_pairs={{0,8},{8,0},{16,24},{24,16},{32,40},{40,32},{48,56},{56,48},{64,72... | collective-permute-start | bytes 786440 | tf_op jit(solution)/shard_map/ppermute | solution.py:16
  386.2 27.9 %collective-permute-start.10 = (bf16[1,1024,256]{2,1,0:T(8,128)(2,1)S(1)}, bf16[1,1024,256]{2,1,0:T(8,128)(2,1)S(1)}, u32[]{:S(2)}, u32[]{:S(2)}) collective-permute-start(bf16[1,1024,256]{2,1,0:T(8,128)(2,1)S(1)} %constant_dynamic-update-slice_fusion.2), channel_id=1, source_target_pairs={{0,16},{8,24},{16,0},{24,8},{32,48},{40,56},{48,32},{56,40},{64,80... | collective-permute-start | bytes 1572872 | tf_op jit(solution)/shard_map/ppermute | solution.py:16
  389.1 31.7 %copy-start.3 = (f32[1024,128]{1,0:T(8,128)S(1)}, f32[1024,128]{1,0:T(8,128)}, u32[]{:S(2)}) copy-start(f32[1024,128]{1,0:T(8,128)} %reduce-scatter.2.cloned.1.call-done) | copy-start | bytes 1572868
  389.1 31.7 %copy-start.4 = (f32[1,128,1024]{2,1,0:T(8,128)S(1)}, f32[1,128,1024]{2,1,0:T(8,128)}, u32[]{:S(2)}) copy-start(f32[1,128,1024]{2,1,0:T(8,128)} %param.11) | copy-start | bytes 1572868
  414.1 53.3 %collective-permute-start.11 = (bf16[1,1024,512]{2,1,0:T(8,128)(2,1)S(1)}, bf16[1,1024,512]{2,1,0:T(8,128)(2,1)S(1)}, u32[]{:S(2)}, u32[]{:S(2)}) collective-permute-start(bf16[1,1024,512]{2,1,0:T(8,128)(2,1)S(1)} %constant_dynamic-update-slice_fusion), channel_id=1, source_target_pairs={{0,32},{8,40},{16,48},{24,56},{32,0},{40,8},{48,16},{56,24},{64,96... | collective-permute-start | bytes 3145736 | tf_op jit(solution)/shard_map/ppermute | solution.py:16
Sparse Core Ops, SparseCore 0:
  134.3 55.4 reduce-scatter.1
